TPU v7x, 32 devices: a whole 2x2x4 slice. The times are simulated.
32 devices in a mesh: grp: 4 (over y, x), seq: 8 (over z, core).
Axes of the slice: x: 2, y: 2, z: 4, core: 2. Of those that a mesh axis runs over, the one named last changes fastest.
Arguments:
- tokens: bfloat16 [2048, 8192], P(None, 'seq'), may hold values from -16 to 16
- proj_weight: bfloat16 [8192, 5120], P('seq', 'grp'), may hold values from -0.0625 to 0.0625
- proj_bias: bfloat16 [5120], P('grp'), may hold values from -3 to 3
- out_weight: bfloat16 [4096, 8192], P('grp'), may hold values from -0.125 to 0.125
- doc_ids: int32 [2048], P('seq'), may hold values from 0 to 2, never falling along the last dimension, each value on 1 to 1280 neighbouring positions
Outputs:
- mixed: bfloat16 [2048, 8192], P('seq', 'grp')
Inputs may be any that keep to these rules, and one draw needn't show every extreme that they name: `doc_ids`: numbers never fall along the sequence; every document has 1 to 1280 tokens, one exactly that many; every number up to 2 is used.
All inputs are finite; a program needn't handle non-finite values.
Results may differ from a plain program's by a relative error of at most 0.012.
Values may be sent and summed in bfloat16 or wider, within the bound.
A program may use at most 256 MiB of HBM per device.

v0:
```python
import functools

import jax
import jax.numpy as jnp
from jax import lax
from jax.experimental import pallas as pl
from jax.experimental.pallas import tpu as pltpu
from jax.sharding import PartitionSpec as P

HEAD_DIM = 128
GQA = 8
MESH = pl.DeviceIdType.MESH

theta_base = 1000000.0
neg_large = -1e30
log2_e = 1.4426950408889634


def layer_kernel(
    line, chunks, rows, width, groups, tiles, wide, slots,
    tok_ref, w_ref, bias_ref, freq_ref, ids_ref, ow_ref,
    out_ref,
    pair_out, pair_in, up_in, dn_in, total, queries, kv_ref, attended, ids_own, ids_col, idall_ref,
    bias, cos_ref, sin_ref, weights, kept, send1, recv1, send2, recv2,
    pair_ss, pair_rs, line_ss, up_rs, dn_rs, id_ss, id_rs, kvl_ss, kvl_rs, kvp_ss, kvp_rs,
    w_sem, ss1, rs1, ss2, rs2,
):
    g = lax.axis_index("grp")
    s = lax.axis_index("seq")
    z, c = s // 2, lax.rem(s, 2)
    n = 2 * line
    partner = s + 1 - 2 * c
    low = z < line // 2
    half = rows // 2
    peer_x = g + 1 - 2 * lax.rem(g, 2)
    peer_y = lax.rem(g + 2, groups)
    passes = 4 * tiles

    def first_peer(t):
        return jnp.where(lax.rem(t, 2) == 0, peer_x, peer_y)

    def second_peer(t):
        return jnp.where(lax.rem(t, 2) == 0, peer_y, peer_x)

    def w_copy(m):
        pos, t = lax.rem(m // tiles, 4), lax.rem(m, tiles)
        block = jnp.where(
            pos == 0, groups - 1 - g, jnp.where(pos == 1, first_peer(t), jnp.where(pos == 2, g, second_peer(t)))
        )
        column = pl.multiple_of((block * tiles + t) * wide, wide)
        slot = lax.rem(m, slots)
        return pltpu.make_async_copy(ow_ref.at[:, pl.ds(column, wide)], weights.at[slot], w_sem.at[slot])

    @pl.loop(0, slots)
    def _(m):
        w_copy(m).start()

    row_ids = jnp.broadcast_to(ids_ref[...].reshape(1, rows), (HEAD_DIM, rows))
    ids_own[...] = row_ids[:8]
    ids_col[...] = row_ids.T
    bias[...] = jnp.broadcast_to(bias_ref[...].astype(jnp.float32), bias.shape)

    barrier = pltpu.get_barrier_semaphore()
    for i in range(1, n):
        pl.semaphore_signal(barrier, inc=1, device_id=(g, lax.rem(s + i, n)), device_id_type=MESH)
    for peer in (peer_x, peer_y):
        pl.semaphore_signal(barrier, inc=1, device_id=(peer, s), device_id_type=MESH)
    pl.semaphore_wait(barrier, n + 1)

    def id_copy(i):
        return pltpu.make_async_remote_copy(
            ids_own, idall_ref.at[s], id_ss.at[i], id_rs.at[i],
            device_id=(g, lax.rem(s + i, n)), device_id_type=MESH,
        )

    def id_wait(i):
        return pltpu.make_async_remote_copy(
            ids_own, idall_ref.at[lax.rem(s + n - i, n)], id_ss.at[i], id_rs.at[i],
            device_id=(g, lax.rem(s + i, n)), device_id_type=MESH,
        )

    idall_ref[s] = ids_own[...]

    def product(kk, dest, core, put):
        row = (2 * dest + core) * rows

        @pl.when(kk == 0)
        def _():
            put(slice(None), jnp.dot(
                tok_ref[pl.ds(pl.multiple_of(row, rows), rows), :], w_ref[:, (chunks - 1) * width :],
                preferred_element_type=jnp.float32,
            ))

        @pl.when(kk > 0)
        def _():
            part = pl.multiple_of(row + (kk - 1) // 2 * half, half)
            column = pl.multiple_of(lax.rem(kk - 1, 2) * 2 * width, 2 * width)
            value = jnp.dot(
                tok_ref[pl.ds(part, half), :], w_ref[:, pl.ds(column, 2 * width)],
                preferred_element_type=jnp.float32,
            )
            put(slice(0, half), value[:, :width])
            put(slice(half, rows), value[:, width:])

    def pair_copy(kk, dest):
        return pltpu.make_async_remote_copy(
            pair_out.at[lax.rem(kk, 2), dest], pair_in.at[kk, dest], pair_ss.at[kk, dest], pair_rs.at[kk, dest],
            device_id=(g, partner), device_id_type=MESH,
        )

    def up_copy(kk, dest):
        return pltpu.make_async_remote_copy(
            pair_in.at[kk, dest], up_in.at[kk, dest], line_ss.at[kk, dest], up_rs.at[kk, dest],
            device_id=(g, lax.rem(s + 2, n)), device_id_type=MESH,
        )

    def dn_copy(kk, dest):
        return pltpu.make_async_remote_copy(
            pair_in.at[kk, dest], dn_in.at[kk, dest], line_ss.at[kk, dest], dn_rs.at[kk, dest],
            device_id=(g, lax.rem(s + n - 2, n)), device_id_type=MESH,
        )

    def kv_line(zz):
        block = kv_ref.at[2 * zz + c]
        return pltpu.make_async_remote_copy(
            block, block, kvl_ss.at[zz], kvl_rs.at[zz], device_id=(g, lax.rem(s + 2, n)), device_id_type=MESH
        )

    def kv_pair(zz):
        block = kv_ref.at[2 * zz + c]
        return pltpu.make_async_remote_copy(
            block, block, kvp_ss.at[zz], kvp_rs.at[zz], device_id=(g, partner), device_id_type=MESH
        )

    def kv_pair_wait(zz):
        block = kv_ref.at[2 * zz + 1 - c]
        return pltpu.make_async_remote_copy(
            block, block, kvp_ss.at[zz], kvp_rs.at[zz], device_id=(g, partner), device_id_type=MESH
        )

    def pair_stage(kk):
        @pl.loop(0, line)
        def _(i):
            dest = jnp.where(low, line - 1 - i, i)

            @pl.when(kk >= 2)
            def _():
                pair_copy(kk - 2, dest).wait_send()

            def put(part, value):
                pair_out[lax.rem(kk, 2), dest, part] = value.astype(jnp.bfloat16)

            product(kk, dest, 1 - c, put)
            pair_copy(kk, dest).start()

    def gathered(kk, dest):
        def put(part, value):
            total[part] = value

        product(kk, dest, c, put)
        pair_copy(kk, dest).wait_recv()
        total[...] += pair_in[kk, dest].astype(jnp.float32)

    def up_stage(kk):
        @pl.loop(0, line - 1 - z)
        def _(d):
            dest = line - 1 - d
            gathered(kk, dest)

            @pl.when(z > 0)
            def _():
                up_copy(kk, dest).wait_recv()
                total[...] += up_in[kk, dest].astype(jnp.float32)

            pair_in[kk, dest] = total[...].astype(jnp.bfloat16)
            up_copy(kk, dest).start()

    def dn_stage(kk):
        @pl.loop(0, z)
        def _(dest):
            gathered(kk, dest)

            @pl.when(z < line - 1)
            def _():
                dn_copy(kk, dest).wait_recv()
                total[...] += dn_in[kk, dest].astype(jnp.float32)

            pair_in[kk, dest] = total[...].astype(jnp.bfloat16)
            dn_copy(kk, dest).start()

    def wait_up_sends(kk):
        @pl.loop(0, line - 1 - z)
        def _(d):
            up_copy(kk, line - 1 - d).wait_send()

    def wait_dn_sends(kk):
        @pl.loop(0, z)
        def _(dest):
            dn_copy(kk, dest).wait_send()

    def rope(x, cosine, sine):
        return x * cosine + pltpu.roll(x, HEAD_DIM // 2, 1) * sine

    def finish(kk):
        gathered(kk, z)

        @pl.when(z > 0)
        def _():
            up_copy(kk, z).wait_recv()
            total[...] += up_in[kk, z].astype(jnp.float32)

        @pl.when(z < line - 1)
        def _():
            dn_copy(kk, z).wait_recv()
            total[...] += dn_in[kk, z].astype(jnp.float32)

        @pl.when(kk == 0)
        def _():
            value = total[...] + bias[:1, (chunks - 1) * width :]
            kv_ref[s, :, :HEAD_DIM] = rope(value[:, :HEAD_DIM], cos_ref[...], sin_ref[...]).astype(jnp.bfloat16)
            kv_ref[s, :, HEAD_DIM:] = value[:, HEAD_DIM:].astype(jnp.bfloat16)
            kv_pair(z).start()

            @pl.when(z < line - 1)
            def _():
                kv_line(z).start()

        @pl.when(kk > 0)
        def _():
            side = (kk - 1) // 2
            group = lax.rem(kk - 1, 2)
            mine = pl.ds(pl.multiple_of(side * half, half), half)
            for i in range(4):
                head = group * 4 + i
                lane = pl.multiple_of(head * HEAD_DIM, HEAD_DIM)
                value = total[(i // 2) * half : (i // 2 + 1) * half, (i % 2) * HEAD_DIM : (i % 2 + 1) * HEAD_DIM]
                value = rope(value + bias[:1, pl.ds(lane, HEAD_DIM)], cos_ref[mine, :], sin_ref[mine, :])
                queries[side, pl.ds(pl.multiple_of(head * half, half), half), :] = value.astype(jnp.bfloat16)

    def relay(h):
        @pl.when(h <= z)
        def _():
            zz = z - h
            kv_line(zz).wait_recv()

            @pl.when(z < line - 1)
            def _():
                kv_line(zz).start()

            kv_pair(zz).start()

    def attend(side):
        ahead = lax.broadcasted_iota(jnp.int32, (half, rows), 1) - lax.broadcasted_iota(jnp.int32, (half, rows), 0)
        ahead = ahead - side * half
        mine_ids = ids_col[pl.ds(pl.multiple_of(side * half, half), half), :1]
        ones = jnp.ones((rows, HEAD_DIM), jnp.bfloat16)
        scale = HEAD_DIM ** (-0.5) * log2_e

        @pl.loop(0, GQA // 4)
        def _(quad):
            tops = [pl.multiple_of((2 * quad + i) * 2 * half, 2 * half) for i in range(2)]
            stacked = [queries[side, pl.ds(top, 2 * half), :] for top in tops]

            def step(j, state):
                keys = kv_ref[j, :, :HEAD_DIM]
                values = jnp.concatenate([kv_ref[j, :, HEAD_DIM:], ones], axis=1)
                allowed = (mine_ids == idall_ref[j, :1, :]) & (ahead <= (s - j) * rows)
                allowed = jnp.concatenate([allowed, allowed], axis=0)
                new = []
                for i in range(2):
                    row_max, weighted = state[i]
                    scores = lax.dot_general(
                        stacked[i], keys, (((1,), (1,)), ((), ())), preferred_element_type=jnp.float32
                    )
                    scores = jnp.where(allowed, scores * scale, neg_large)
                    new_max = jnp.maximum(row_max, jnp.max(scores, axis=1, keepdims=True))
                    exps = jnp.exp2(scores - new_max)
                    update = jnp.dot(exps.astype(jnp.bfloat16), values, preferred_element_type=jnp.float32)
                    new.append((new_max, weighted * jnp.exp2(row_max - new_max) + update))
                return tuple(new)

            initial = (
                jnp.full((2 * half, 1), neg_large, jnp.float32),
                jnp.zeros((2 * half, 2 * HEAD_DIM), jnp.float32),
            )
            state = lax.fori_loop(0, s + 1, step, (initial, initial))
            for i in range(2):
                weighted = state[i][1]
                value = (weighted[:, :HEAD_DIM] / weighted[:, HEAD_DIM:]).astype(jnp.bfloat16)
                for part in range(2):
                    lane = pl.multiple_of((4 * quad + 2 * i + part) * HEAD_DIM, HEAD_DIM)
                    attended[side, :, pl.ds(lane, HEAD_DIM)] = value[part * half : (part + 1) * half]

    def mixed(side, pos, t):
        m = side * passes + pos * tiles + t
        w_copy(m).wait()
        value = jnp.dot(attended[side], weights[lax.rem(m, slots)], preferred_element_type=jnp.float32)

        @pl.when(m + slots < 2 * passes)
        def _():
            w_copy(m + slots).start()

        return value

    def copy1(side, slot, t):
        return pltpu.make_async_remote_copy(
            send1.at[side, slot, t], recv1.at[side, slot, t], ss1.at[side, slot, t], rs1.at[side, slot, t],
            device_id=(first_peer(t), s), device_id_type=MESH,
        )

    def copy2(side, t):
        return pltpu.make_async_remote_copy(
            send2.at[side, t], recv2.at[side, t], ss2.at[side, t], rs2.at[side, t],
            device_id=(second_peer(t), s), device_id_type=MESH,
        )

    def send_out(side):
        @pl.loop(0, 2 * tiles)
        def _(m):
            slot, t = m // tiles, lax.rem(m, tiles)
            send1[side, slot, t] = mixed(side, slot, t).astype(jnp.bfloat16)
            copy1(side, slot, t).start()

    def pass_on(side):
        @pl.loop(0, tiles)
        def _(t):
            kept[side, t] = mixed(side, 2, t)

        @pl.loop(0, tiles)
        def _(t):
            value = mixed(side, 3, t)
            copy1(side, 0, t).wait_recv()
            send2[side, t] = (value + recv1[side, 0, t].astype(jnp.float32)).astype(jnp.bfloat16)
            copy2(side, t).start()

    def collect(side):
        @pl.loop(0, tiles)
        def _(t):
            copy1(side, 1, t).wait_recv()
            copy2(side, t).wait_recv()
            value = kept[side, t] + recv1[side, 1, t].astype(jnp.float32) + recv2[side, t].astype(jnp.float32)
            mine = pl.ds(pl.multiple_of(side * half, half), half)
            out_ref[mine, pl.ds(pl.multiple_of(t * wide, wide), wide)] = value.astype(jnp.bfloat16)

    def primary(kk):
        @pl.when(low)
        def _():
            up_stage(kk)

        @pl.when(jnp.logical_not(low))
        def _():
            dn_stage(kk)

    def secondary(kk):
        @pl.when(low)
        def _():
            dn_stage(kk)

        @pl.when(jnp.logical_not(low))
        def _():
            up_stage(kk)

    def wait_primary(kk):
        @pl.when(low)
        def _():
            wait_up_sends(kk)

        @pl.when(jnp.logical_not(low))
        def _():
            wait_dn_sends(kk)

    def wait_secondary(kk):
        @pl.when(low)
        def _():
            wait_dn_sends(kk)

        @pl.when(jnp.logical_not(low))
        def _():
            wait_up_sends(kk)

    pair_stage(0)
    for i in range(1, n):
        id_copy(i).start()

    @pl.loop(0, chunks)
    def _(kk):
        @pl.when(kk >= 2)
        def _():
            wait_primary(kk - 2)

        primary(kk)

        @pl.when(kk + 1 < chunks)
        def _():
            pair_stage(kk + 1)

        @pl.when(kk >= 1)
        def _():
            secondary(kk - 1)

        @pl.when(kk == 1)
        def _():
            angles = (s * rows + lax.broadcasted_iota(jnp.int32, (rows, HEAD_DIM), 0)).astype(
                jnp.float32
            ) * freq_ref[...]
            lane = lax.broadcasted_iota(jnp.int32, (rows, HEAD_DIM), 1)
            sine = jnp.sin(angles)
            cos_ref[...] = jnp.cos(angles)
            sin_ref[...] = jnp.where(lane < HEAD_DIM // 2, -sine, sine)

        @pl.when(kk >= 2)
        def _():
            finish(kk - 2)

    for i in range(1, n):
        id_copy(i).wait_send()
        id_wait(i).wait_recv()

    @pl.loop(1, line)
    def _(h):
        relay(h)

    @pl.loop(0, z + 1)
    def _(zz):
        kv_pair_wait(zz).wait_recv()

    @pl.loop(0, 2)
    def _(side):
        attend(side)
        send_out(side)

        @pl.when(side == 0)
        def _():
            secondary(chunks - 1)
            finish(chunks - 2)

        pass_on(side)

        @pl.when(side == 0)
        def _():
            finish(chunks - 1)

    @pl.loop(0, 2)
    def _(side):
        collect(side)

    @pl.loop(0, chunks)
    def _(kk):
        @pl.when(kk >= chunks - 2)
        def _():
            wait_primary(kk)

            @pl.loop(0, line)
            def _(dest):
                pair_copy(kk, dest).wait_send()

        wait_secondary(kk)

    @pl.loop(0, z + 1)
    def _(zz):
        kv_pair(zz).wait_send()

        @pl.when(z < line - 1)
        def _():
            kv_line(zz).wait_send()

    @pl.loop(0, 2)
    def _(side):
        @pl.loop(0, tiles)
        def _(t):
            copy1(side, 0, t).wait_send()
            copy1(side, 1, t).wait_send()
            copy2(side, t).wait_send()


def body(seq, groups, tokens, proj_weight, proj_bias, out_weight, doc_ids):
    rows = doc_ids.shape[0]
    columns = proj_weight.shape[1]
    width = 2 * HEAD_DIM
    chunks = columns // width
    line = seq // 2
    half = rows // 2
    q_width = GQA * HEAD_DIM
    block = out_weight.shape[1] // groups
    wide = 4 * HEAD_DIM
    tiles = block // wide
    slots = 2 * tiles
    inverse_freq = theta_base ** (-(jnp.arange(HEAD_DIM // 2, dtype=jnp.float32) * 2.0) / HEAD_DIM)
    freq = jnp.concatenate([inverse_freq, inverse_freq])[None, :]
    vmem = pl.BlockSpec(memory_space=pltpu.VMEM)
    dma = pltpu.SemaphoreType.DMA
    bf16, f32, i32 = jnp.bfloat16, jnp.float32, jnp.int32

    return pl.pallas_call(
        functools.partial(layer_kernel, line, chunks, rows, width, groups, tiles, wide, slots),
        out_shape=jax.ShapeDtypeStruct((rows, block), bf16),
        in_specs=[vmem] * 5 + [pl.BlockSpec(memory_space=pl.ANY)],
        out_specs=vmem,
        scratch_shapes=[
            pltpu.VMEM((2, line, rows, width), bf16),
            pltpu.VMEM((chunks, line, rows, width), bf16),
            pltpu.VMEM((chunks, line, rows, width), bf16),
            pltpu.VMEM((chunks, line, rows, width), bf16),
            pltpu.VMEM((rows, width), f32),
            pltpu.VMEM((2, GQA * half, HEAD_DIM), bf16),
            pltpu.VMEM((seq, rows, width), bf16),
            pltpu.VMEM((2, half, q_width), bf16),
            pltpu.VMEM((8, rows), i32),
            pltpu.VMEM((rows, HEAD_DIM), i32),
            pltpu.VMEM((seq, 8, rows), i32),
            pltpu.VMEM((8, columns), f32),
            pltpu.VMEM((rows, HEAD_DIM), f32),
            pltpu.VMEM((rows, HEAD_DIM), f32),
            pltpu.VMEM((slots, q_width, wide), bf16),
            pltpu.VMEM((2, tiles, half, wide), f32),
            pltpu.VMEM((2, 2, tiles, half, wide), bf16),
            pltpu.VMEM((2, 2, tiles, half, wide), bf16),
            pltpu.VMEM((2, tiles, half, wide), bf16),
            pltpu.VMEM((2, tiles, half, wide), bf16),
        ]
        + [dma((chunks, line))] * 5
        + [dma((seq,))] * 2
        + [dma((line,))] * 4
        + [dma((slots,)), dma((2, 2, tiles)), dma((2, 2, tiles)), dma((2, tiles)), dma((2, tiles))],
        compiler_params=pltpu.CompilerParams(
            collective_id=0, has_side_effects=True, vmem_limit_bytes=67043328
        ),
        name="layer",
    )(tokens, proj_weight, proj_bias[None, :], freq, doc_ids[None, :], out_weight)


def solution(mesh):
    return jax.shard_map(
        functools.partial(body, mesh.shape["seq"], mesh.shape["grp"]),
        mesh=mesh,
        in_specs=(P(None, "seq"), P("seq", "grp"), P("grp"), P("grp", None), P("seq")),
        out_specs=P("seq", "grp"),
        check_vma=False,
    )
```

profile of v0, /device:TPU:25, one launch (start us, length us, event | category | flops | bytes accessed | tf_op | source)
XLA Modules:
  0.0 115.6 jit_solution(12669828141544647040)
XLA Ops:
  0.0 0.7 maximum_bitcast_fusion.freq_ref
  0.7 1.3 %broadcast_in_dim.9.bias_ref = bf16[1,1280]{1,0:T(2,128)(2,1)} reshape(bf16[1280]{0:T(1024)(128)(2,1)} %param.7) | data formatting | bytes 5120 | tf_op jit(solution)/shard_map/broadcast_in_dim | solution.py:529
  2.0 111.3 %layer.1 = bf16[256,2048]{1,0:T(8,128)(2,1)} custom-call(bf16[2048,1024]{1,0:T(8,128)(2,1)} %tok_ref.1, bf16[1024,1280]{1,0:T(8,128)(2,1)} %w_ref.1, bf16[1,1280]{1,0:T(2,128)(2,1)} %broadcast_in_dim.9.bias_ref, f32[1,128]{1,0:T(1,128)} %maximum_bitcast_fusion.freq_ref, s32[1,256]{1,0:T(1,128)} %bitcast.3, bf16[1024,8192]{1,0:T(8,128)(2,1)} %ow_ref.1), custom_call_target="tpu_custom_call" | custom-call | tf_op jit(solution)/shard_map/layer/pallas_call | solution.py:494
  113.3 2.3 %copy.7 = bf16[256,2048]{1,0:T(8,128)(2,1)} copy(bf16[256,2048]{1,0:T(8,128)(2,1)} %layer.1) | data formatting | bytes 2097152
  (1 shorter events, 0.0 us)
where the time goes:
time: 116 us
  Pallas kernels  111 us (96%)
  local copies, waits for them, and re-layouts  3.59 us (3%)
    pallas_call x1, Pallas kernels, body(): pl.pallas_call(functools.partial(layer_kernel, line, chunks, rows, width,...  111 us

commit v1 on v0

v1 whole, which is shorter than its diff:
```python
import functools

import jax
import jax.numpy as jnp
from jax import lax
from jax.experimental import pallas as pl
from jax.experimental.pallas import tpu as pltpu
from jax.sharding import PartitionSpec as P

HEAD_DIM = 128
GQA = 8
PIECES = 4
MESH = pl.DeviceIdType.MESH

theta_base = 1000000.0
neg_large = -1e30
log2_e = 1.4426950408889634


def layer_kernel(
    line, rows, width, groups, tiles, wide, slots,
    tok_ref, w_ref, bias_ref, freq_ref, ids_ref, ow_ref,
    out_ref,
    kpair_out, kpair_in, kline_in, qpair_out, qpair_in, qline_in, ktotal, qtotal,
    queries, kv_ref, attended, ids_col, idall_ref, bias, cos_ref, sin_ref,
    weights, kept, send1, recv1, send2, recv2,
    kpair_ss, kpair_rs, kline_ss, kline_rs, qpair_ss, qpair_rs, qline_ss, qline_rs,
    idl_ss, idl_rs, idp_ss, idp_rs, kvu_ss, kvd_ss, kvl_rs, kvp_ss, kvp_rs,
    w_sem, ss1, rs1, ss2, rs2,
):
    g = lax.axis_index("grp")
    s = lax.axis_index("seq")
    z, c = s // 2, lax.rem(s, 2)
    n = 2 * line
    partner = s + 1 - 2 * c
    above = lax.rem(s + 2, n)
    below = lax.rem(s + n - 2, n)
    low = z < line // 2
    inner = (z > 0) & (z < line - 1)
    hub = line // 2 - 1
    pieces = PIECES
    part = rows // pieces
    q_width = GQA * HEAD_DIM
    peer_x = g + 1 - 2 * lax.rem(g, 2)
    peer_y = lax.rem(g + 2, groups)
    passes = 4 * tiles
    resident = slots == passes
    bf16, f32 = jnp.bfloat16, jnp.float32

    def first_peer(t):
        return jnp.where(lax.rem(t, 2) == 0, peer_x, peer_y)

    def second_peer(t):
        return jnp.where(lax.rem(t, 2) == 0, peer_y, peer_x)

    def w_copy(m):
        pos, t = lax.rem(m // tiles, 4), lax.rem(m, tiles)
        block = jnp.where(
            pos == 0, groups - 1 - g, jnp.where(pos == 1, first_peer(t), jnp.where(pos == 2, g, second_peer(t)))
        )
        column = pl.multiple_of((block * tiles + t) * wide, wide)
        slot = lax.rem(m, slots)
        return pltpu.make_async_copy(ow_ref.at[:, pl.ds(column, wide)], weights.at[slot], w_sem.at[slot])

    @pl.loop(0, slots)
    def _(m):
        w_copy(m).start()

    barrier = pltpu.get_barrier_semaphore()
    for peer in ((g, partner), (peer_x, s), (peer_y, s)):
        pl.semaphore_signal(barrier, inc=1, device_id=peer, device_id_type=MESH)

    @pl.when(z < line - 1)
    def _():
        pl.semaphore_signal(barrier, inc=1, device_id=(g, above), device_id_type=MESH)

    @pl.when(z > 0)
    def _():
        pl.semaphore_signal(barrier, inc=1, device_id=(g, below), device_id_type=MESH)

    row_ids = jnp.broadcast_to(ids_ref[...].reshape(1, rows), (HEAD_DIM, rows))
    idall_ref[s] = row_ids[:8]
    ids_col[...] = row_ids.T
    bias[...] = jnp.broadcast_to(bias_ref[...].astype(f32), bias.shape)
    pl.semaphore_wait(barrier, 3 + (z > 0).astype(jnp.int32) + (z < line - 1).astype(jnp.int32))

    def remote(src, dst, ss, rs, peer):
        return pltpu.make_async_remote_copy(src, dst, ss, rs, device_id=peer, device_id_type=MESH)


    def kpair_copy(dest):
        return remote(kpair_out.at[dest], kpair_in.at[dest], kpair_ss.at[dest], kpair_rs.at[dest], (g, partner))

    def qpair_copy(p, dest):
        slot = lax.rem(p, 2)
        return remote(
            qpair_out.at[slot, dest], qpair_in.at[p, dest], qpair_ss.at[p, dest], qpair_rs.at[p, dest], (g, partner)
        )

    def kline_copy(up, dest):
        return remote(
            kpair_in.at[dest], kline_in.at[up, dest], kline_ss.at[dest], kline_rs.at[up, dest],
            (g, jnp.where(up == 1, above, below)),
        )

    def qline_copy(up, p, dest):
        return remote(
            qpair_in.at[p, dest], qline_in.at[p, dest + up], qline_ss.at[p, dest], qline_rs.at[p, dest + up],
            (g, jnp.where(up == 1, above, below)),
        )

    def kproduct(dest, core):
        row = pl.multiple_of((2 * dest + core) * rows, rows)
        return jnp.dot(tok_ref[pl.ds(row, rows), :], w_ref[:, q_width:], preferred_element_type=f32)

    def q_tokens(p, dest, core):
        return tok_ref[pl.ds(pl.multiple_of((2 * dest + core) * rows + p * part, part), part), :]

    def kpair_stage():
        @pl.loop(0, line)
        def _(i):
            dest = jnp.where(low, line - 1 - i, i)
            kpair_out[dest] = kproduct(dest, 1 - c).astype(bf16)
            kpair_copy(dest).start()

    def qpair_stage(p):
        @pl.loop(0, line // 4)
        def _(b):
            stacked = jnp.concatenate([q_tokens(p, 4 * b + i, 1 - c) for i in range(4)], axis=0)
            value = jnp.dot(stacked, w_ref[:, :q_width], preferred_element_type=f32).astype(bf16)

            @pl.when(p >= 2)
            def _():
                for i in range(4):
                    qpair_copy(p - 2, 4 * b + i).wait_send()

            for i in range(4):
                qpair_out[lax.rem(p, 2), 4 * b + i] = value[i * part : (i + 1) * part]
                qpair_copy(p, 4 * b + i).start()

    def kline_stage(up, enabled):
        count = jnp.where(up == 1, jnp.where(z < hub, line, line - 1 - z), jnp.where(z > hub, z, 0))

        @pl.loop(0, jnp.where(enabled, count, 0))
        def _(i):
            dest = jnp.where(up == 1, line - 1 - i, i)
            ktotal[...] = kproduct(dest, c)
            kpair_copy(dest).wait_recv()
            source = jnp.where(up == 1, z > 0, z < line - 1)

            @pl.when(source)
            def _():
                kline_copy(up, dest).wait_recv()
                kpair_in[dest] = (ktotal[...] + kpair_in[dest].astype(f32) + kline_in[up, dest].astype(f32)).astype(bf16)

            @pl.when(jnp.logical_not(source))
            def _():
                kpair_in[dest] = (ktotal[...] + kpair_in[dest].astype(f32)).astype(bf16)

            kline_copy(up, dest).start()

    def qline_stage(up, p, enabled):
        @pl.loop(0, jnp.where(enabled, jnp.where(up == 1, line - 1 - z, z), 0))
        def _(i):
            dest = jnp.where(up == 1, line - 1 - i, i)
            qtotal[...] = jnp.dot(q_tokens(p, dest, c), w_ref[:, :q_width], preferred_element_type=f32)
            qpair_copy(p, dest).wait_recv()
            source = jnp.where(up == 1, z > 0, z < line - 1)

            @pl.when(source)
            def _():
                qline_copy(up, p, dest).wait_recv()
                qpair_in[p, dest] = (
                    qtotal[...] + qpair_in[p, dest].astype(f32) + qline_in[p, dest + up].astype(f32)
                ).astype(bf16)

            @pl.when(jnp.logical_not(source))
            def _():
                qpair_in[p, dest] = (qtotal[...] + qpair_in[p, dest].astype(f32)).astype(bf16)

            qline_copy(up, p, dest).start()

    main = low.astype(jnp.int32)
    other = 1 - main
    end = jnp.logical_not(inner)


    def tables(slot, block):
        angles = (block * rows + lax.broadcasted_iota(jnp.int32, (rows, HEAD_DIM), 0)).astype(f32) * freq_ref[...]
        lane = lax.broadcasted_iota(jnp.int32, (rows, HEAD_DIM), 1)
        sine = jnp.sin(angles)
        cos_ref[slot] = jnp.cos(angles)
        sin_ref[slot] = jnp.where(lane < HEAD_DIM // 2, -sine, sine)

    def rope(x, cosine, sine):
        return x * cosine + pltpu.roll(x, HEAD_DIM // 2, 1) * sine


    def kv_up(zz):
        block = kv_ref.at[2 * zz + c]
        return remote(block, block, kvu_ss.at[zz], kvl_rs.at[zz], (g, above))

    def kv_down(zz):
        block = kv_ref.at[2 * zz + c]
        return remote(block, block, kvd_ss.at[zz], kvl_rs.at[zz], (g, below))

    def kv_pair(zz, core):
        block = kv_ref.at[2 * zz + core]
        return remote(block, block, kvp_ss.at[zz], kvp_rs.at[zz], (g, partner))

    def kv_finish(zz, slot):
        ktotal[...] = kproduct(zz, c)
        kpair_copy(zz).wait_recv()
        ktotal[...] += kpair_in[zz].astype(f32)

        @pl.when(z < line - 1)
        def _():
            kline_copy(0, zz).wait_recv()
            ktotal[...] += kline_in[0, zz].astype(f32)

        kline_copy(1, zz).wait_recv()
        value = ktotal[...] + kline_in[1, zz].astype(f32) + bias[:1, q_width:]
        kv_ref[2 * zz + c, :, :HEAD_DIM] = rope(value[:, :HEAD_DIM], cos_ref[slot], sin_ref[slot]).astype(bf16)
        kv_ref[2 * zz + c, :, HEAD_DIM:] = value[:, HEAD_DIM:].astype(bf16)

        @pl.when(z < line - 1)
        def _():
            kv_up(zz).start()

        @pl.when(zz < z)
        def _():
            kv_down(zz).start()

        kv_pair(zz, c).start()

    def kv_relay():
        @pl.loop(0, jnp.where(z > hub, z, 0))
        def _(i):
            zz = z - 1 - i
            kv_up(zz).wait_recv()

            @pl.when(z < line - 1)
            def _():
                kv_up(zz).start()

            kv_pair(zz, c).start()

        @pl.loop(0, jnp.where(z < hub, z + 1, 0))
        def _(i):
            zz = z - i
            kv_down(zz).wait_recv()

            @pl.when(zz < z)
            def _():
                kv_down(zz).start()

            kv_pair(zz, c).start()


    def id_up(zz):
        block = idall_ref.at[2 * zz + c]
        return remote(block, block, idl_ss.at[zz], idl_rs.at[zz], (g, above))

    def id_pair(zz, core):
        block = idall_ref.at[2 * zz + core]
        return remote(block, block, idp_ss.at[zz], idp_rs.at[zz], (g, partner))

    def id_send(zz):
        @pl.when(z < line - 1)
        def _():
            id_up(zz).start()

        id_pair(zz, c).start()

    def id_relay():
        @pl.loop(0, z)
        def _(i):
            zz = z - 1 - i
            id_up(zz).wait_recv()
            id_send(zz)


    def finish(p):
        qtotal[...] = jnp.dot(q_tokens(p, z, c), w_ref[:, :q_width], preferred_element_type=f32)
        qpair_copy(p, z).wait_recv()
        qtotal[...] += qpair_in[p, z].astype(f32)

        @pl.when(z < line - 1)
        def _():
            qline_copy(0, p, z).wait_recv()
            qtotal[...] += qline_in[p, z].astype(f32)

        @pl.when(z > 0)
        def _():
            qline_copy(1, p, z).wait_recv()
            qtotal[...] += qline_in[p, z + 1].astype(f32)

        mine = pl.ds(pl.multiple_of(p * part, part), part)
        cosine, sine = cos_ref[0, mine, :], sin_ref[0, mine, :]
        for head in range(GQA):
            lanes = slice(head * HEAD_DIM, (head + 1) * HEAD_DIM)
            value = rope(qtotal[:, lanes] + bias[:1, lanes], cosine, sine)
            queries[head * part : (head + 1) * part, :] = value.astype(bf16)

    def attend(p):
        heads = GQA // 2
        ahead = lax.broadcasted_iota(jnp.int32, (part, rows), 1) - lax.broadcasted_iota(jnp.int32, (part, rows), 0)
        ahead = ahead - p * part
        mine_ids = ids_col[pl.ds(pl.multiple_of(p * part, part), part), :1]
        ones = jnp.ones((rows, HEAD_DIM), bf16)
        scale = HEAD_DIM ** (-0.5) * log2_e
        stacked = [queries[i * heads * part : (i + 1) * heads * part, :] for i in range(2)]

        def step(j, state):
            keys = kv_ref[j, :, :HEAD_DIM]
            values = jnp.concatenate([kv_ref[j, :, HEAD_DIM:], ones], axis=1)
            allowed = (mine_ids == idall_ref[j, :1, :]) & (ahead <= (s - j) * rows)
            allowed = jnp.concatenate([allowed] * heads, axis=0)
            new = []
            for i in range(2):
                row_max, weighted = state[i]
                scores = lax.dot_general(
                    stacked[i], keys, (((1,), (1,)), ((), ())), preferred_element_type=f32
                )
                scores = jnp.where(allowed, scores * scale, neg_large)
                new_max = jnp.maximum(row_max, jnp.max(scores, axis=1, keepdims=True))
                exps = jnp.exp2(scores - new_max)
                update = jnp.dot(exps.astype(bf16), values, preferred_element_type=f32)
                new.append((new_max, weighted * jnp.exp2(row_max - new_max) + update))
            return tuple(new)

        initial = (
            jnp.full((heads * part, 1), neg_large, f32),
            jnp.zeros((heads * part, 2 * HEAD_DIM), f32),
        )
        state = lax.fori_loop(jnp.maximum(s - (line + 1), 0), s + 1, step, (initial, initial))
        for i in range(2):
            weighted = state[i][1]
            value = (weighted[:, :HEAD_DIM] / weighted[:, HEAD_DIM:]).astype(bf16)
            for h in range(heads):
                head = i * heads + h
                attended[:, head * HEAD_DIM : (head + 1) * HEAD_DIM] = value[h * part : (h + 1) * part]


    def mixed(p, pos, t):
        m = p * passes + pos * tiles + t
        slot = lax.rem(m, slots)
        if resident:
            @pl.when(p == 0)
            def _():
                w_copy(m).wait()
        else:
            w_copy(m).wait()
        value = jnp.dot(attended[...], weights[slot], preferred_element_type=f32)
        if not resident:
            @pl.when(m + slots < pieces * passes)
            def _():
                w_copy(m + slots).start()
        return value

    def copy1(p, slot, t):
        return remote(
            send1.at[p, slot, t], recv1.at[p, slot, t], ss1.at[p, slot, t], rs1.at[p, slot, t], (first_peer(t), s)
        )

    def copy2(p, t):
        return remote(send2.at[p, t], recv2.at[p, t], ss2.at[p, t], rs2.at[p, t], (second_peer(t), s))

    def send_out(p):
        @pl.loop(0, 2 * tiles)
        def _(m):
            slot, t = m // tiles, lax.rem(m, tiles)
            send1[p, slot, t] = mixed(p, slot, t).astype(bf16)
            copy1(p, slot, t).start()

    def pass_on(p):
        @pl.loop(0, tiles)
        def _(t):
            kept[lax.rem(p, 2), t] = mixed(p, 2, t)

        @pl.loop(0, tiles)
        def _(t):
            value = mixed(p, 3, t)
            copy1(p, 0, t).wait_recv()
            send2[p, t] = (value + recv1[p, 0, t].astype(f32)).astype(bf16)
            copy2(p, t).start()

    def collect(p):
        mine = pl.ds(pl.multiple_of(p * part, part), part)

        @pl.loop(0, tiles)
        def _(t):
            copy1(p, 1, t).wait_recv()
            copy2(p, t).wait_recv()
            value = kept[lax.rem(p, 2), t] + recv1[p, 1, t].astype(f32) + recv2[p, t].astype(f32)
            out_ref[mine, pl.ds(pl.multiple_of(t * wide, wide), wide)] = value.astype(bf16)

    id_send(z)
    kpair_stage()
    kline_stage(main, end)
    qpair_stage(0)
    qline_stage(main, 0, end)
    tables(0, s)
    id_relay()
    kline_stage(main, inner)
    kline_stage(other, True)

    @pl.when(z >= hub)
    def _():
        kv_finish(z, 0)

    @pl.loop(0, jnp.where(z == hub, hub, 0))
    def _(i):
        zz = hub - 1 - i
        tables(1, 2 * zz + c)
        kv_finish(zz, 1)

    kv_relay()

    @pl.loop(0, z + 1)
    def _(zz):
        id_pair(zz, 1 - c).wait_recv()

    @pl.loop(0, z + 1)
    def _(zz):
        kv_pair(zz, 1 - c).wait_recv()

    @pl.loop(0, pieces + 2)
    def _(p):
        more = p + 1 < pieces
        here = p < pieces

        @pl.when(more)
        def _():
            qpair_stage(p + 1)

        @pl.when((p >= 1) & (p <= pieces))
        def _():
            attend(p - 1)
            send_out(p - 1)

        qline_stage(main, p + 1, more & end)
        qline_stage(main, p, here & inner)

        @pl.when((p >= 1) & (p <= pieces))
        def _():
            pass_on(p - 1)

        qline_stage(other, p, here)

        @pl.when(p >= 2)
        def _():
            collect(p - 2)

        @pl.when(here)
        def _():
            finish(p)


    @pl.loop(0, line)
    def _(dest):
        kpair_copy(dest).wait_send()
        sent = jnp.where(jnp.maximum(dest, hub) == z, 0, 1)

        @pl.when(sent == 1)
        def _():
            kline_copy(jnp.where(jnp.maximum(dest, hub) > z, 1, 0), dest).wait_send()

        @pl.loop(0, pieces)
        def _(p):
            @pl.when(p >= pieces - 2)
            def _():
                qpair_copy(p, dest).wait_send()

            @pl.when(dest != z)
            def _():
                qline_copy(jnp.where(dest > z, 1, 0), p, dest).wait_send()

    @pl.loop(0, z + 1)
    def _(zz):
        id_pair(zz, c).wait_send()
        kv_pair(zz, c).wait_send()

        @pl.when(z < line - 1)
        def _():
            id_up(zz).wait_send()

        @pl.when((z < line - 1) & (z >= hub))
        def _():
            kv_up(zz).wait_send()

        @pl.when((zz < z) & (z <= hub))
        def _():
            kv_down(zz).wait_send()

    @pl.loop(0, pieces)
    def _(p):
        @pl.loop(0, tiles)
        def _(t):
            copy1(p, 0, t).wait_send()
            copy1(p, 1, t).wait_send()
            copy2(p, t).wait_send()


def body(seq, groups, tokens, proj_weight, proj_bias, out_weight, doc_ids):
    rows = doc_ids.shape[0]
    columns = proj_weight.shape[1]
    width = 2 * HEAD_DIM
    line = seq // 2
    part = rows // PIECES
    q_width = GQA * HEAD_DIM
    block = out_weight.shape[1] // groups
    wide = 4 * HEAD_DIM
    tiles = block // wide
    slots = 4 * tiles if line <= 4 else 2 * tiles
    inverse_freq = theta_base ** (-(jnp.arange(HEAD_DIM // 2, dtype=jnp.float32) * 2.0) / HEAD_DIM)
    freq = jnp.concatenate([inverse_freq, inverse_freq])[None, :]
    vmem = pl.BlockSpec(memory_space=pltpu.VMEM)
    dma = pltpu.SemaphoreType.DMA
    bf16, f32, i32 = jnp.bfloat16, jnp.float32, jnp.int32

    return pl.pallas_call(
        functools.partial(layer_kernel, line, rows, width, groups, tiles, wide, slots),
        out_shape=jax.ShapeDtypeStruct((rows, block), bf16),
        in_specs=[vmem] * 5 + [pl.BlockSpec(memory_space=pl.ANY)],
        out_specs=vmem,
        scratch_shapes=[
            pltpu.VMEM((line, rows, width), bf16),
            pltpu.VMEM((line, rows, width), bf16),
            pltpu.VMEM((2, line, rows, width), bf16),
            pltpu.VMEM((2, line, part, q_width), bf16),
            pltpu.VMEM((PIECES, line, part, q_width), bf16),
            pltpu.VMEM((PIECES, line + 1, part, q_width), bf16),
            pltpu.VMEM((rows, width), f32),
            pltpu.VMEM((part, q_width), f32),
            pltpu.VMEM((GQA * part, HEAD_DIM), bf16),
            pltpu.VMEM((seq, rows, width), bf16),
            pltpu.VMEM((part, q_width), bf16),
            pltpu.VMEM((rows, HEAD_DIM), i32),
            pltpu.VMEM((seq, 8, rows), i32),
            pltpu.VMEM((8, columns), f32),
            pltpu.VMEM((2, rows, HEAD_DIM), f32),
            pltpu.VMEM((2, rows, HEAD_DIM), f32),
            pltpu.VMEM((slots, q_width, wide), bf16),
            pltpu.VMEM((2, tiles, part, wide), f32),
            pltpu.VMEM((PIECES, 2, tiles, part, wide), bf16),
            pltpu.VMEM((PIECES, 2, tiles, part, wide), bf16),
            pltpu.VMEM((PIECES, tiles, part, wide), bf16),
            pltpu.VMEM((PIECES, tiles, part, wide), bf16),
        ]
        + [dma((line,)), dma((line,)), dma((line,)), dma((2, line))]
        + [dma((PIECES, line)), dma((PIECES, line)), dma((PIECES, line)), dma((PIECES, line + 1))]
        + [dma((line,))] * 9
        + [dma((slots,)), dma((PIECES, 2, tiles)), dma((PIECES, 2, tiles)), dma((PIECES, tiles)), dma((PIECES, tiles))],
        compiler_params=pltpu.CompilerParams(
            collective_id=0, has_side_effects=True, vmem_limit_bytes=67043328
        ),
        name="layer",
    )(tokens, proj_weight, proj_bias[None, :], freq, doc_ids[None, :], out_weight)


def solution(mesh):
    return jax.shard_map(
        functools.partial(body, mesh.shape["seq"], mesh.shape["grp"]),
        mesh=mesh,
        in_specs=(P(None, "seq"), P("seq", "grp"), P("grp"), P("grp", None), P("seq")),
        out_specs=P("seq", "grp"),
        check_vma=False,
    )
```

time: 116 us -> 100 us (0.86)
  Pallas kernels: 111 us -> 96 us
    pallas_call x1, Pallas kernels: 111 us -> 96 us  [body(): pl.pallas_call(functools.partial(layer_kernel, line, rows, width, groups,...]
where the time goes in v1:
time: 100 us
  Pallas kernels  96 us (96%)
  local copies, waits for them, and re-layouts  3.59 us (4%)
    pallas_call x1, Pallas kernels, body(): pl.pallas_call(functools.partial(layer_kernel, line, rows, width, groups,...  96 us
    unnamed x1, local copies, waits for them, and re-layouts  2.3 us

profile of v1, /device:TPU:25, one launch (start us, length us, event | category | flops | bytes accessed | tf_op | source)
XLA Modules:
  0.0 100.3 jit_solution(12148411163718678458)
XLA Ops:
  0.0 0.7 maximum_bitcast_fusion.freq_ref
  0.7 1.3 %broadcast_in_dim.9.bias_ref = bf16[1,1280]{1,0:T(2,128)(2,1)} reshape(bf16[1280]{0:T(1024)(128)(2,1)} %param.7) | data formatting | bytes 5120 | tf_op jit(solution)/shard_map/broadcast_in_dim | solution.py:559
  2.0 96.0 %layer.1 = bf16[256,2048]{1,0:T(8,128)(2,1)} custom-call(bf16[2048,1024]{1,0:T(8,128)(2,1)} %tok_ref.1, bf16[1024,1280]{1,0:T(8,128)(2,1)} %w_ref.1, bf16[1,1280]{1,0:T(2,128)(2,1)} %broadcast_in_dim.9.bias_ref, f32[1,128]{1,0:T(1,128)} %maximum_bitcast_fusion.freq_ref, s32[1,256]{1,0:T(1,128)} %bitcast.3, bf16[1024,8192]{1,0:T(8,128)(2,1)} %ow_ref.1), custom_call_target="tpu_custom_call" | custom-call | tf_op jit(solution)/shard_map/layer/pallas_call | solution.py:522
  98.0 2.3 %copy.7 = bf16[256,2048]{1,0:T(8,128)(2,1)} copy(bf16[256,2048]{1,0:T(8,128)(2,1)} %layer.1) | data formatting | bytes 2097152
  (1 shorter events, 0.0 us)

commit v2 on v1

v2 whole, which is shorter than its diff:
```python
import functools

import jax
import jax.numpy as jnp
import numpy as np
from jax import lax
from jax.experimental import pallas as pl
from jax.experimental.pallas import tpu as pltpu
from jax.sharding import PartitionSpec as P

HEAD_DIM = 128
GQA = 8
PARTS = (1, 1, 1, 1)
SPLITS = (2, 2, 2, 2)
MESH = pl.DeviceIdType.MESH

theta_base = 1000000.0
neg_large = -1e30
log2_e = 1.4426950408889634


def layer_kernel(
    line, rows, width, groups, tiles, wide, slots,
    bias_ref, freq_ref, ids_ref, tok_hbm, w_hbm, ow_ref,
    out_hbm,
    tok_ref, w_ref, kpair_out, kpair_in, kline_in, qpair_out, qpair_in, qline_in, ktotal, qtotal,
    queries, kv_ref, score_ref, attended, ids_col, idall_ref, first_ref, place_ref, bias, cos_ref, sin_ref,
    out_ref, weights, kept, own, send1, recv1, send2, recv2, tok_sem, in_sem, out_sem,
    kpair_ss, kpair_rs, kline_ss, kline_rs, qpair_ss, qpair_rs, qline_ss, qline_rs,
    idl_ss, idl_rs, idp_ss, idp_rs, kvu_ss, kvd_ss, kvl_rs, kvp_ss, kvp_rs,
    w_sem, ss1, rs1, ss2, rs2,
):
    g = lax.axis_index("grp")
    s = lax.axis_index("seq")
    z, c = s // 2, lax.rem(s, 2)
    n = 2 * line
    partner = s + 1 - 2 * c
    above = lax.rem(s + 2, n)
    below = lax.rem(s + n - 2, n)
    low = z < line // 2
    inner = (z > 0) & (z < line - 1)
    hub = line // 2 - 1
    pieces = len(PARTS)
    heights = [rows * k // sum(PARTS) for k in PARTS]
    starts = [sum(heights[:p]) for p in range(pieces)]
    span = line + 2
    batch = max(k for k in range(1, 7) if span % k == 0)
    steps = span // batch
    q_width = GQA * HEAD_DIM
    peer_x = g + 1 - 2 * lax.rem(g, 2)
    peer_y = lax.rem(g + 2, groups)
    passes = 4 * tiles
    resident = slots == passes
    bf16, f32 = jnp.bfloat16, jnp.float32

    def first_peer(t):
        return jnp.where(lax.rem(t, 2) == 0, peer_x, peer_y)

    def second_peer(t):
        return jnp.where(lax.rem(t, 2) == 0, peer_y, peer_x)

    def w_copy(m):
        pos, t = lax.rem(m // tiles, 4), lax.rem(m, tiles)
        block = jnp.where(
            pos == 0, groups - 1 - g, jnp.where(pos == 1, first_peer(t), jnp.where(pos == 2, g, second_peer(t)))
        )
        column = pl.multiple_of((block * tiles + t) * wide, wide)
        slot = lax.rem(m, slots)
        return pltpu.make_async_copy(ow_ref.at[:, pl.ds(column, wide)], weights.at[slot], w_sem.at[slot])

    def tok_copy(block):
        mine = pl.ds(pl.multiple_of(block * rows, rows), rows)
        return pltpu.make_async_copy(tok_hbm.at[mine, :], tok_ref.at[mine, :], tok_sem.at[block])

    kv_columns = pltpu.make_async_copy(w_hbm.at[:, q_width:], w_ref.at[:, q_width:], in_sem.at[0])
    q_columns = pltpu.make_async_copy(w_hbm.at[:, :q_width], w_ref.at[:, :q_width], in_sem.at[1])

    def far_first(i):
        return jnp.where(low, line - 1 - i, i)

    kv_columns.start()
    for core in (1 - c, c):
        @pl.loop(0, line)
        def _(i):
            tok_copy(2 * far_first(i) + core).start()

    q_columns.start()
    barrier = pltpu.get_barrier_semaphore()
    for peer in ((g, partner), (peer_x, s), (peer_y, s)):
        pl.semaphore_signal(barrier, inc=1, device_id=peer, device_id_type=MESH)

    @pl.when(z < line - 1)
    def _():
        pl.semaphore_signal(barrier, inc=1, device_id=(g, above), device_id_type=MESH)

    @pl.when(z > 0)
    def _():
        pl.semaphore_signal(barrier, inc=1, device_id=(g, below), device_id_type=MESH)

    row_ids = jnp.broadcast_to(ids_ref[...].reshape(1, rows), (HEAD_DIM, rows))
    idall_ref[s] = row_ids[:8]
    ids_col[...] = row_ids.T
    bias[...] = jnp.broadcast_to(bias_ref[...].astype(f32), bias.shape)
    pl.semaphore_wait(barrier, 3 + (z > 0).astype(jnp.int32) + (z < line - 1).astype(jnp.int32))

    def remote(src, dst, ss, rs, peer):
        return pltpu.make_async_remote_copy(src, dst, ss, rs, device_id=peer, device_id_type=MESH)


    def kpair_copy(dest):
        return remote(kpair_out.at[dest], kpair_in.at[dest], kpair_ss.at[dest], kpair_rs.at[dest], (g, partner))

    def rows_of(p):
        return pl.ds(starts[p], heights[p])

    def qpair_copy(p, dest):
        return remote(
            qpair_out.at[p % 2, dest, : heights[p]], qpair_in.at[dest, rows_of(p)],
            qpair_ss.at[p, dest], qpair_rs.at[p, dest], (g, partner),
        )

    def kline_copy(up, dest):
        return remote(
            kpair_in.at[dest], kline_in.at[up, dest], kline_ss.at[dest], kline_rs.at[up, dest],
            (g, jnp.where(up == 1, above, below)),
        )

    def strip_of(p, h):
        size = heights[p] // SPLITS[p]
        return pl.ds(starts[p] + h * size, size)

    def qline_copy(up, p, dest, h):
        return remote(
            qpair_in.at[dest, strip_of(p, h)], qline_in.at[dest + up, strip_of(p, h)],
            qline_ss.at[p, dest, h], qline_rs.at[p, dest + up, h], (g, jnp.where(up == 1, above, below)),
        )

    def kproduct(dest, core):
        row = pl.multiple_of((2 * dest + core) * rows, rows)
        return jnp.dot(tok_ref[pl.ds(row, rows), :], w_ref[:, q_width:], preferred_element_type=f32)

    def q_tokens(p, dest, core):
        return tok_ref[pl.ds(pl.multiple_of((2 * dest + core) * rows + starts[p], heights[0]), heights[p]), :]

    def kpair_stage():
        @pl.loop(0, line)
        def _(i):
            dest = far_first(i)
            tok_copy(2 * dest + 1 - c).wait()
            kpair_out[dest] = kproduct(dest, 1 - c).astype(bf16)
            kpair_copy(dest).start()

    def q_product(p, b, core):
        stacked = jnp.concatenate([q_tokens(p, 4 * b + i, core) for i in range(4)], axis=0)
        return jnp.dot(stacked, w_ref[:, :q_width], preferred_element_type=f32)

    def qpair_stage(p):
        height = heights[p]

        @pl.loop(0, line // 4)
        def _(b):
            if p >= 2:
                for i in range(4):
                    qpair_copy(p - 2, 4 * b + i).wait_send()
            value = q_product(p, b, 1 - c).astype(bf16)
            for i in range(4):
                qpair_out[p % 2, 4 * b + i, :height] = value[i * height : (i + 1) * height]
                qpair_copy(p, 4 * b + i).start()

    def qown_stage(p):
        height = heights[p]

        @pl.loop(0, line // 4)
        def _(b):
            qtotal[: 4 * height] = q_product(p, b, c)
            for i in range(4):
                dest = 4 * b + i
                qpair_copy(p, dest).wait_recv()
                qpair_in[dest, rows_of(p)] = (
                    qtotal[i * height : (i + 1) * height] + qpair_in[dest, rows_of(p)].astype(f32)
                ).astype(bf16)

    def kline_stage(up, enabled):
        count = jnp.where(up == 1, jnp.where(z < hub, line, line - 1 - z), jnp.where(z > hub, z, 0))

        @pl.loop(0, jnp.where(enabled, count, 0))
        def _(i):
            dest = jnp.where(up == 1, line - 1 - i, i)
            ktotal[...] = kproduct(dest, c)
            kpair_copy(dest).wait_recv()
            source = jnp.where(up == 1, z > 0, z < line - 1)

            @pl.when(source)
            def _():
                kline_copy(up, dest).wait_recv()
                kpair_in[dest] = (ktotal[...] + kpair_in[dest].astype(f32) + kline_in[up, dest].astype(f32)).astype(bf16)

            @pl.when(jnp.logical_not(source))
            def _():
                kpair_in[dest] = (ktotal[...] + kpair_in[dest].astype(f32)).astype(bf16)

            kline_copy(up, dest).start()

    def qline_stage(up, p, enabled):
        @pl.loop(0, jnp.where(enabled, jnp.where(up == 1, line - 1 - z, z), 0))
        def _(i):
            dest = jnp.where(up == 1, line - 1 - i, i)

            for h in range(SPLITS[p]):
                @pl.when(jnp.where(up == 1, z > 0, z < line - 1))
                def _(h=h):
                    strip = strip_of(p, h)
                    qline_copy(up, p, dest, h).wait_recv()
                    qpair_in[dest, strip] = (
                        qpair_in[dest, strip].astype(f32) + qline_in[dest + up, strip].astype(f32)
                    ).astype(bf16)

                qline_copy(up, p, dest, h).start()

    main = low.astype(jnp.int32)
    other = 1 - main
    end = jnp.logical_not(inner)


    def tables(slot, block):
        angles = (block * rows + lax.broadcasted_iota(jnp.int32, (rows, HEAD_DIM), 0)).astype(f32) * freq_ref[...]
        lane = lax.broadcasted_iota(jnp.int32, (rows, HEAD_DIM), 1)
        sine = jnp.sin(angles)
        cos_ref[slot] = jnp.cos(angles)
        sin_ref[slot] = jnp.where(lane < HEAD_DIM // 2, -sine, sine)

    def rope(x, cosine, sine):
        return x * cosine + pltpu.roll(x, HEAD_DIM // 2, 1) * sine


    def kv_up(zz):
        block = kv_ref.at[2 * zz + c]
        return remote(block, block, kvu_ss.at[zz], kvl_rs.at[zz], (g, above))

    def kv_down(zz):
        block = kv_ref.at[2 * zz + c]
        return remote(block, block, kvd_ss.at[zz], kvl_rs.at[zz], (g, below))

    def kv_pair(zz, core):
        block = kv_ref.at[2 * zz + core]
        return remote(block, block, kvp_ss.at[zz], kvp_rs.at[zz], (g, partner))

    def kv_finish(zz, slot):
        ktotal[...] = kproduct(zz, c)
        kpair_copy(zz).wait_recv()
        ktotal[...] += kpair_in[zz].astype(f32)

        @pl.when(z < line - 1)
        def _():
            kline_copy(0, zz).wait_recv()
            ktotal[...] += kline_in[0, zz].astype(f32)

        kline_copy(1, zz).wait_recv()
        value = ktotal[...] + kline_in[1, zz].astype(f32) + bias[:1, q_width:]
        kv_ref[2 * zz + c, :rows, :] = rope(value[:, :HEAD_DIM], cos_ref[slot], sin_ref[slot]).astype(bf16)
        for i in range(rows // HEAD_DIM):
            turned = value[i * HEAD_DIM : (i + 1) * HEAD_DIM, HEAD_DIM:].T
            kv_ref[2 * zz + c, rows + i * HEAD_DIM : rows + (i + 1) * HEAD_DIM, :] = turned.astype(bf16)

        @pl.when(z < line - 1)
        def _():
            kv_up(zz).start()

        @pl.when(zz < z)
        def _():
            kv_down(zz).start()

        kv_pair(zz, c).start()

    def kv_relay(begin, end):
        @pl.loop(begin, jnp.where(z > hub, jnp.minimum(z, end), begin))
        def _(i):
            zz = z - 1 - i
            kv_up(zz).wait_recv()

            @pl.when(z < line - 1)
            def _():
                kv_up(zz).start()

            kv_pair(zz, c).start()

    def kv_lower():
        @pl.loop(0, jnp.where(z < hub, z + 1, 0))
        def _(i):
            zz = z - i
            kv_down(zz).wait_recv()

            @pl.when(zz < z)
            def _():
                kv_down(zz).start()

            kv_pair(zz, c).start()


    def id_up(zz):
        block = idall_ref.at[2 * zz + c]
        return remote(block, block, idl_ss.at[zz], idl_rs.at[zz], (g, above))

    def id_pair(zz, core):
        block = idall_ref.at[2 * zz + core]
        return remote(block, block, idp_ss.at[zz], idp_rs.at[zz], (g, partner))

    def id_send(zz):
        @pl.when(z < line - 1)
        def _():
            id_up(zz).start()

        id_pair(zz, c).start()

    def id_relay():
        @pl.loop(0, z)
        def _(i):
            zz = z - 1 - i
            id_up(zz).wait_recv()
            id_send(zz)


    def finish(p):
        height = heights[p]
        cosine, sine = cos_ref[0, rows_of(p), :], sin_ref[0, rows_of(p), :]

        @pl.when(z < line - 1)
        def _():
            for h in range(SPLITS[p]):
                qline_copy(0, p, z, h).wait_recv()

        @pl.when(z > 0)
        def _():
            for h in range(SPLITS[p]):
                qline_copy(1, p, z, h).wait_recv()

        def turn(sources):
            for head in range(GQA):
                lanes = slice(head * HEAD_DIM, (head + 1) * HEAD_DIM)
                value = qpair_in[z, rows_of(p), lanes].astype(f32) + bias[:1, lanes]
                for source in sources:
                    value = value + qline_in[source, rows_of(p), lanes].astype(f32)
                queries[head * height : (head + 1) * height, :] = rope(value, cosine, sine).astype(bf16)

        @pl.when(inner)
        def _():
            turn((z, z + 1))

        @pl.when(z == 0)
        def _():
            turn((z,))

        @pl.when(z == line - 1)
        def _():
            turn((z + 1,))


    def places():
        @pl.loop(0, z + 1)
        def _(zz):
            id_pair(zz, 1 - c).wait_recv()

        def step(j, count):
            return count + jnp.where(idall_ref[j, :1, :] < ids_col[:, :1], 1.0, 0.0)

        count = lax.fori_loop(0, s + 1, step, jnp.zeros((rows, rows), f32))
        first = jnp.broadcast_to(jnp.sum(count, axis=1, keepdims=True), (rows, HEAD_DIM))
        first = jnp.concatenate(
            [first[i * HEAD_DIM : (i + 1) * HEAD_DIM].T for i in range(rows // HEAD_DIM)], axis=1
        )[:8].astype(jnp.int32)
        place = s * rows + lax.broadcasted_iota(jnp.int32, (8, rows), 1)
        for p in range(pieces):
            lanes = slice(starts[p], starts[p] + heights[p])
            first_ref[p] = jnp.concatenate([first[:, lanes]] * (rows // heights[p]), axis=1)
            place_ref[p] = jnp.concatenate([place[:, lanes]] * (rows // heights[p]), axis=1)

    def attend(p):
        height = heights[p]
        heads = rows // height
        stacks = GQA // heads
        lanes = rows
        key = lax.broadcasted_iota(jnp.int32, (rows, lanes), 0)
        ones = jnp.ones((16, rows), bf16)
        scale = HEAD_DIM ** (-0.5) * log2_e
        start = s - (line + 1)

        def step(k, state):
            highest = [state[i][0] for i in range(stacks)]
            for n in range(batch):
                j = start + k * batch + n
                block = jnp.maximum(j, 0)
                keys = kv_ref[block, :rows, :]
                allowed = (key >= first_ref[p, :1, :] - j * rows) & (key <= place_ref[p, :1, :] - j * rows)
                for i in range(stacks):
                    scores = lax.dot_general(
                        keys, queries[i * lanes : (i + 1) * lanes, :], (((1,), (1,)), ((), ())),
                        preferred_element_type=f32,
                    )
                    scores = jnp.where(allowed, scores * scale, neg_large)
                    score_ref[i, n * rows : (n + 1) * rows, :] = scores
                    highest[i] = jnp.maximum(highest[i], jnp.max(scores.reshape(rows // 8, 8, lanes), axis=0))
            new = []
            for i in range(stacks):
                row_max, weighted = state[i]
                new_max = jnp.broadcast_to(jnp.max(highest[i], axis=0, keepdims=True), (8, lanes))
                update = jnp.zeros((HEAD_DIM + 16, lanes), f32)
                for n in range(batch):
                    block = jnp.maximum(start + k * batch + n, 0)
                    turned = [
                        kv_ref[block, rows + m * HEAD_DIM : rows + (m + 1) * HEAD_DIM, :] for m in range(rows // HEAD_DIM)
                    ]
                    values = jnp.concatenate([jnp.concatenate(turned, axis=1), ones], axis=0)
                    exps = jnp.exp2(score_ref[i, n * rows : (n + 1) * rows, :] - new_max[:1])
                    update = update + jnp.dot(values, exps.astype(bf16), preferred_element_type=f32)
                if steps > 1:
                    update = weighted * jnp.exp2(row_max[:1] - new_max[:1]) + update
                new.append((new_max, update))
            return tuple(new)

        initial = (jnp.full((8, lanes), neg_large, f32), jnp.zeros((HEAD_DIM + 16, lanes), f32))
        if steps > 1:
            state = lax.fori_loop(0, steps, step, (initial,) * stacks)
        else:
            state = step(0, (initial,) * stacks)
        for i in range(stacks):
            weighted = state[i][1]
            value = weighted[:HEAD_DIM] / weighted[HEAD_DIM : HEAD_DIM + 1]
            for k in range(lanes // HEAD_DIM):
                block = value[:, k * HEAD_DIM : (k + 1) * HEAD_DIM].T.astype(bf16)
                for h in range(HEAD_DIM // height):
                    head = i * heads + k * (HEAD_DIM // height) + h
                    attended[:height, head * HEAD_DIM : (head + 1) * HEAD_DIM] = block[h * height : (h + 1) * height]


    def mixed(p, pos, t):
        m = p * passes + pos * tiles + t
        slot = lax.rem(m, slots)
        if not resident:
            w_copy(m).wait()
        value = jnp.dot(attended[: heights[p]], weights[slot], preferred_element_type=f32)
        if not resident:
            @pl.when(m + slots < pieces * passes)
            def _():
                w_copy(m + slots).start()
        return value

    def mixed_tiles(p, pos, begin, count):
        if not resident:
            return [mixed(p, pos, begin + i) for i in range(count)]
        joined = jnp.concatenate([weights[pos * tiles + begin + i] for i in range(count)], axis=1)
        value = jnp.dot(attended[: heights[p]], joined, preferred_element_type=f32)
        return [value[:, i * wide : (i + 1) * wide] for i in range(count)]

    def copy1(p, slot, t):
        return remote(
            send1.at[slot, t, rows_of(p)], recv1.at[slot, t, rows_of(p)], ss1.at[p, slot, t], rs1.at[p, slot, t], (first_peer(t), s)
        )

    def copy2(p, t):
        return remote(send2.at[t, rows_of(p)], recv2.at[t, rows_of(p)], ss2.at[p, t], rs2.at[p, t], (second_peer(t), s))

    def send_out(p):
        if resident and p == 0:
            @pl.loop(0, slots)
            def _(m):
                w_copy(m).wait()

        @pl.loop(0, 2)
        def _(slot):
            for begin in range(0, tiles, 2):
                for i, value in enumerate(mixed_tiles(p, slot, begin, 2)):
                    send1[slot, begin + i, rows_of(p)] = value.astype(bf16)
                    copy1(p, slot, begin + i).start()

    def pass_on(p):
        for begin in range(0, tiles, 4):
            for i, value in enumerate(mixed_tiles(p, 2, begin, 4)):
                kept[begin + i, rows_of(p)] = value
        for begin in range(0, tiles, 4):
            for i, value in enumerate(mixed_tiles(p, 3, begin, 4)):
                own[begin + i, : heights[p]] = value

        @pl.loop(0, tiles)
        def _(t):
            copy1(p, 0, t).wait_recv()
            send2[t, rows_of(p)] = (own[t, : heights[p]] + recv1[0, t, rows_of(p)].astype(f32)).astype(bf16)
            copy2(p, t).start()

    def out_copy(p):
        return pltpu.make_async_copy(out_ref.at[rows_of(p), :], out_hbm.at[rows_of(p), :], out_sem.at[p])

    def collect(p):
        @pl.loop(0, tiles)
        def _(t):
            copy1(p, 1, t).wait_recv()
            copy2(p, t).wait_recv()
            value = kept[t, rows_of(p)] + recv1[1, t, rows_of(p)].astype(f32) + recv2[t, rows_of(p)].astype(f32)
            out_ref[rows_of(p), pl.ds(pl.multiple_of(t * wide, wide), wide)] = value.astype(bf16)

        out_copy(p).start()

    def settle():
        @pl.loop(0, line)
        def _(dest):
            kpair_copy(dest).wait_send()
            sent = jnp.where(jnp.maximum(dest, hub) == z, 0, 1)

            @pl.when(sent == 1)
            def _():
                kline_copy(jnp.where(jnp.maximum(dest, hub) > z, 1, 0), dest).wait_send()

            for p in range(pieces):
                if p >= pieces - 2:
                    qpair_copy(p, dest).wait_send()

                @pl.when(dest != z)
                def _(p=p):
                    for h in range(SPLITS[p]):
                        qline_copy(jnp.where(dest > z, 1, 0), p, dest, h).wait_send()

        @pl.loop(0, z + 1)
        def _(zz):
            id_pair(zz, c).wait_send()
            kv_pair(zz, c).wait_send()

            @pl.when(z < line - 1)
            def _():
                id_up(zz).wait_send()

            @pl.when((z < line - 1) & (z >= hub))
            def _():
                kv_up(zz).wait_send()

            @pl.when((zz < z) & (z <= hub))
            def _():
                kv_down(zz).wait_send()

    def query_stage(p):
        qown_stage(p)
        qline_stage(main, p, end)

    id_send(z)
    kv_columns.wait()
    kpair_stage()

    @pl.loop(0, line)
    def _(dest):
        tok_copy(2 * dest + c).wait()

    kline_stage(main, end)
    q_columns.wait()

    @pl.loop(0, slots)
    def _(m):
        w_copy(m).start()

    qpair_stage(0)
    qpair_stage(1)
    query_stage(0)
    id_relay()
    kline_stage(main, inner)
    kline_stage(other, True)

    for p in range(1, pieces):
        if p + 1 < pieces:
            qpair_stage(p + 1)
        query_stage(p)

    @pl.loop(0, jnp.where(z == hub, 2, 1))
    def _(i):
        tables(i, jnp.where(i == 0, s, s - 2))

    places()

    @pl.when(z >= hub)
    def _():
        kv_finish(z, 0)

    @pl.loop(0, jnp.where(z == hub, hub, 0))
    def _(i):
        zz = hub - 1 - i

        @pl.when(i > 0)
        def _():
            tables(1, 2 * zz + c)

        kv_finish(zz, 1)

    kv_relay(0, 1)
    qline_stage(main, 0, inner)
    kv_relay(1, line)
    kv_lower()

    @pl.loop(0, z + 1)
    def _(zz):
        kv_pair(zz, 1 - c).wait_recv()

    for p in range(pieces + 2):
        here = p < pieces
        relay = here and p > 0
        if relay:
            qline_stage(main, p, inner & jnp.logical_not(low))
        if 1 <= p <= pieces:
            attend(p - 1)
            send_out(p - 1)
        if relay:
            qline_stage(main, p, inner & low)
        if here:
            qline_stage(other, p, True)
        if p == pieces:
            settle()
        if 1 <= p <= pieces:
            pass_on(p - 1)
        if p >= 2:
            collect(p - 2)
        if here:
            finish(p)


    for p in range(pieces):
        @pl.loop(0, tiles)
        def _(t):
            copy1(p, 0, t).wait_send()
            copy1(p, 1, t).wait_send()
            copy2(p, t).wait_send()

        out_copy(p).wait()


def body(seq, groups, tokens, proj_weight, proj_bias, out_weight, doc_ids):
    rows = doc_ids.shape[0]
    columns = proj_weight.shape[1]
    width = 2 * HEAD_DIM
    line = seq // 2
    part = rows * max(PARTS) // sum(PARTS)
    pieces = len(PARTS)
    q_width = GQA * HEAD_DIM
    block = out_weight.shape[1] // groups
    wide = 4 * HEAD_DIM
    tiles = block // wide
    slots = 4 * tiles if line <= 4 else 2 * tiles
    inverse_freq = (theta_base ** (-np.arange(HEAD_DIM // 2) * 2.0 / HEAD_DIM)).astype(np.float32)
    freq = jnp.asarray(np.concatenate([inverse_freq, inverse_freq])[None, :])
    vmem = pl.BlockSpec(memory_space=pltpu.VMEM)
    dma = pltpu.SemaphoreType.DMA
    bf16, f32, i32 = jnp.bfloat16, jnp.float32, jnp.int32

    return pl.pallas_call(
        functools.partial(layer_kernel, line, rows, width, groups, tiles, wide, slots),
        out_shape=jax.ShapeDtypeStruct((rows, block), bf16),
        in_specs=[vmem] * 3 + [pl.BlockSpec(memory_space=pl.ANY)] * 3,
        out_specs=pl.BlockSpec(memory_space=pl.ANY),
        scratch_shapes=[
            pltpu.VMEM(tokens.shape, bf16),
            pltpu.VMEM(proj_weight.shape, bf16),
            pltpu.VMEM((line, rows, width), bf16),
            pltpu.VMEM((line, rows, width), bf16),
            pltpu.VMEM((2, line, rows, width), bf16),
            pltpu.VMEM((2, line, part, q_width), bf16),
            pltpu.VMEM((line, rows, q_width), bf16),
            pltpu.VMEM((line + 1, rows, q_width), bf16),
            pltpu.VMEM((rows, width), f32),
            pltpu.VMEM((4 * part, q_width), f32),
            pltpu.VMEM((GQA * part, HEAD_DIM), bf16),
            pltpu.VMEM((seq, 2 * rows, HEAD_DIM), bf16),
            pltpu.VMEM((GQA * part // rows, 6 * rows, rows), f32),
            pltpu.VMEM((part, q_width), bf16),
            pltpu.VMEM((rows, HEAD_DIM), i32),
            pltpu.VMEM((seq, 8, rows), i32),
            pltpu.VMEM((pieces, 8, rows), i32),
            pltpu.VMEM((pieces, 8, rows), i32),
            pltpu.VMEM((8, columns), f32),
            pltpu.VMEM((2, rows, HEAD_DIM), f32),
            pltpu.VMEM((2, rows, HEAD_DIM), f32),
            pltpu.VMEM((rows, block), bf16),
            pltpu.VMEM((slots, q_width, wide), bf16),
            pltpu.VMEM((tiles, rows, wide), f32),
            pltpu.VMEM((tiles, part, wide), f32),
            pltpu.VMEM((2, tiles, rows, wide), bf16),
            pltpu.VMEM((2, tiles, rows, wide), bf16),
            pltpu.VMEM((tiles, rows, wide), bf16),
            pltpu.VMEM((tiles, rows, wide), bf16),
        ]
        + [dma((seq,)), dma((2,)), dma((pieces,))]
        + [dma((line,)), dma((line,)), dma((line,)), dma((2, line))]
        + [dma((pieces, line)), dma((pieces, line)), dma((pieces, line, 2)), dma((pieces, line + 1, 2))]
        + [dma((line,))] * 9
        + [dma((slots,)), dma((pieces, 2, tiles)), dma((pieces, 2, tiles)), dma((pieces, tiles)), dma((pieces, tiles))],
        compiler_params=pltpu.CompilerParams(
            collective_id=0, has_side_effects=True, vmem_limit_bytes=67043328
        ),
        name="layer",
    )(proj_bias, freq, doc_ids[None, :], tokens, proj_weight, out_weight)


def solution(mesh):
    return jax.shard_map(
        functools.partial(body, mesh.shape["seq"], mesh.shape["grp"]),
        mesh=mesh,
        in_specs=(P(None, "seq"), P("seq", "grp"), P("grp"), P("grp", None), P("seq")),
        out_specs=P("seq", "grp"),
        check_vma=False,
    )
```

time: 100 us -> 76.4 us (0.76)
  the two profiles are of different devices: /device:TPU:25 before, /device:TPU:0 now
where the time goes in v2:
time: 76.4 us; the launch traced here: 76.2 us
  Pallas kernels  73.9 us (97%)
  local copies, waits for them, and re-layouts  2.3 us (3%)
    pallas_call x1, Pallas kernels, body(): pl.pallas_call(functools.partial(layer_kernel, line, rows, width, groups,...  73.9 us
    unnamed x1, local copies, waits for them, and re-layouts  2.3 us

profile of v2, /device:TPU:0, one launch (start us, length us, event | category | flops | bytes accessed | tf_op | source)
XLA Modules:
  0.0 76.2 jit_solution(1455532737330638997)
XLA Ops:
  0.0 73.9 %layer.1 = bf16[256,2048]{1,0:T(8,128)(2,1)} custom-call(bf16[1280]{0:T(1024)(128)(2,1)} %bias_ref.1, f32[1,128]{1,0:T(1,128)} %constant.2.clone.freq_ref, s32[1,256]{1,0:T(1,128)} %bitcast.1, bf16[2048,1024]{1,0:T(8,128)(2,1)} %tok_hbm.1, bf16[1024,1280]{1,0:T(8,128)(2,1)} %w_hbm.1, bf16[1024,8192]{1,0:T(8,128)(2,1)} %ow_ref.1), custom_call_target="tpu_custom_call" | custom-call | tf_op jit(solution)/shard_map/layer/pallas_call | solution.py:648
  73.9 2.3 %copy.8 = bf16[256,2048]{1,0:T(8,128)(2,1)} copy(bf16[256,2048]{1,0:T(8,128)(2,1)} %layer.1) | data formatting | bytes 2097152
